TPU v7x, 256 devices: a whole 4x4x8 slice. The times are simulated.
256 devices in a mesh: row: 8 (over y, core), th: 8 (over z), ph: 4 (over x).
Axes of the slice: x: 4, y: 4, z: 8, core: 2. Of those that a mesh axis runs over, the one named last changes fastest.
Arguments:
- fields: float32 [6, 128, 128, 512], P(None, 'row', 'th', 'ph'), may hold values from -6 to 6
- lapse_field: float32 [128, 128, 512], P('row', 'th', 'ph'), may hold values from 0.3 to 1
- excision: int32 [128, 128, 512], P('row', 'th', 'ph'), may hold values 0 or 1
- sample_cells: int32 [128, 128, 4], P('row', 'th', 'ph'), may hold values from 0 to 127
- old_basis: float32 [252, 196608], P(None, ('row', 'th', 'ph'))
Outputs:
- new_fields: float32 [6, 128, 128, 512], P(None, 'row', 'th', 'ph')
- basis_out: float32 [256, 196608], P(None, ('row', 'th', 'ph'))
- factor: float32 [256, 256], replicated
Inputs may be any that keep to these rules, and one draw needn't show every extreme that they name: `excision`: 1 marks an excised cell.
All inputs are finite; a program needn't handle non-finite values. No bound on the sum of `excision` on one device may be relied on, other than what follows from the above.
Results may differ from a plain program's by a relative error of at most 0.007.
Values sent between devices are 32-bit elements; how exact they have to be, the bound alone decides.
A program may use at most 64 MiB of HBM per device.

v0:
```python
import math
import jax
import jax.numpy as jnp
from jax import lax
from jax.sharding import PartitionSpec as P

SPACING = 128
damping_rate = 3.0
time_step = 0.3
azimuth_gain = 5.0


def with_halo(block, sides, width, periodic):
    for axis, dim in sides:
        count = lax.axis_size(axis)
        forward = [(i, i + 1) for i in range(count - 1)]
        if periodic:
            forward.append((count - 1, 0))
        backward = [(target, source) for source, target in forward]
        low = lax.ppermute(
            lax.slice_in_dim(block, block.shape[dim] - width, None, axis=dim), axis, forward
        )
        high = lax.ppermute(lax.slice_in_dim(block, 0, width, axis=dim), axis, backward)
        block = jnp.concatenate([low, block, high], axis=dim)
    return block


def shifted(padded, axis_dim, offset):
    lengths = [padded.shape[0] - 4, padded.shape[1] - 4, padded.shape[2] - 4]
    starts = [2, 2, 2]
    starts[axis_dim] = 2 + offset
    return padded[
        starts[0] : starts[0] + lengths[0],
        starts[1] : starts[1] + lengths[1],
        starts[2] : starts[2] + lengths[2],
    ]


def derivative(padded, axis_dim):
    near_diff = shifted(padded, axis_dim, 1) - shifted(padded, axis_dim, -1)
    far_diff = shifted(padded, axis_dim, 2) - shifted(padded, axis_dim, -2)
    spacing_gain = azimuth_gain if axis_dim == 2 else 1.0
    return (8.0 * near_diff - far_diff) * (spacing_gain / 12.0)


def curl_of(padded, start_comp):
    first_part = padded[start_comp]
    second_part = padded[start_comp + 1]
    third_part = padded[start_comp + 2]
    return jnp.stack(
        [
            derivative(third_part, 1) - derivative(second_part, 2),
            derivative(first_part, 2) - derivative(third_part, 0),
            derivative(second_part, 0) - derivative(first_part, 1),
        ]
    )


def rates(padded, fields, damping):
    electric = curl_of(padded, 3) - damping_rate * damping * fields[:3]
    magnetic = -curl_of(padded, 0) - damping_rate * damping * fields[3:]
    return jnp.concatenate([electric, magnetic])


def padded_each(product):
    beside_all = with_halo(product, (("ph", 3),), 2, True)
    return with_halo(beside_all, (("row", 1), ("th", 2)), 2, False)


def on_device(fields, lapse_field, excision, sample_cells, old_basis):
    damping = excision.astype(jnp.float32)
    rad_cells = fields.shape[1]
    pol_cells = fields.shape[2]
    azi_cells = fields.shape[3]
    rad_total = rad_cells * lax.axis_size("row")
    pol_total = pol_cells * lax.axis_size("th")
    section_one = fields + time_step * rates(padded_each(lapse_field * fields), fields, damping)
    rate_two = rates(padded_each(lapse_field * section_one), section_one, damping)
    new_fields = 0.5 * (fields + section_one + time_step * rate_two)
    rad_index = (lax.axis_index("row") * rad_cells + jnp.arange(rad_cells)).astype(jnp.float32)
    pol_index = (lax.axis_index("th") * pol_cells + jnp.arange(pol_cells)).astype(jnp.float32)
    radius = 1.0 + 2.0 * (rad_index + 0.5) / rad_total
    polar = jnp.pi * (pol_index + 0.5) / pol_total
    weight = radius[:, None] * jnp.sqrt(jnp.sin(polar))[None, :]
    groups = azi_cells // SPACING
    chosen = jnp.arange(SPACING)[None, None, None, :] == sample_cells[:, :, :, None]
    weighted = jnp.where(chosen, weight[:, :, None, None], 0.0)

    def sample(field_set):
        grouped = field_set.reshape(6, rad_cells, pol_cells, groups, SPACING)
        return jnp.sum(grouped * weighted[None], axis=-1)

    snap_one = sample(section_one)
    snap_two = sample(new_fields)
    snapshot = jnp.stack(
        [
            snap_one[:3].reshape(-1),
            snap_one[3:].reshape(-1),
            snap_two[:3].reshape(-1),
            snap_two[3:].reshape(-1),
        ]
    )
    matrix = jnp.concatenate([old_basis, snapshot], axis=0)
    gram_sum = lax.psum(
        jnp.dot(matrix, matrix.T, precision=lax.Precision.HIGHEST), ("row", "th", "ph")
    )
    factor_low = lax.linalg.cholesky(gram_sum)
    solved = lax.linalg.triangular_solve(factor_low, matrix, left_side=True, lower=True)
    row_scale = math.sqrt(
        old_basis.shape[1] * lax.axis_size("row") * lax.axis_size("th") * lax.axis_size("ph")
    )
    return (new_fields, solved * row_scale, factor_low.T / row_scale)


def solution(mesh):
    return jax.shard_map(
        on_device,
        mesh=mesh,
        in_specs=(
            P(None, "row", "th", "ph"),
            P("row", "th", "ph"),
            P("row", "th", "ph"),
            P("row", "th", "ph"),
            P(None, ("row", "th", "ph")),
        ),
        out_specs=(P(None, "row", "th", "ph"), P(None, ("row", "th", "ph")), P()),
        check_vma=False,
    )
```

profile of v0, /device:TPU:2, one launch (start us, length us, event | category | flops | bytes accessed | tf_op | source)
XLA Modules:
  0.0 412.0 jit_solution(14045041573448911381)
XLA Ops:
  9.3 1.6 collective-permute-start
  12.3 1.9 collective-permute-done
  14.9 1.3 collective-permute-done.1
  17.0 1.3 collective-permute-start.2
  19.7 3.8 collective-permute-done.3
  24.2 3.8 collective-permute-start.4
  29.3 2.4 collective-permute-done.4
  31.7 4.4 %collective-permute-done.5 = f32[6,20,2,132]{3,2,1,0:T(2,128)S(1)} collective-permute-done((f32[6,20,2,132]{3,2,1,0:T(2,128)S(1)}, f32[6,20,2,132]{3,2,1,0:T(2,128)S(1)}, u32[]{:S(2)}, u32[]{:S(2)}) %collective-permute-start.5) | collective-permute-done | bytes 126752 | tf_op jit(solution)/shard_map/ppermute | solution.py:23
  44.3 1.9 collective-permute-done.6
  48.9 3.4 collective-permute-start.8
  53.6 6.2 %collective-permute-done.9 = f32[6,2,16,132]{3,2,1,0:T(8,128)S(1)} collective-permute-done((f32[6,2,16,132]{3,2,1,0:T(8,128)S(1)}, f32[6,2,16,132]{3,2,1,0:T(8,128)S(1)}, u32[]{:S(2)}, u32[]{:S(2)}) %collective-permute-start.9) | collective-permute-done | bytes 101408 | tf_op jit(solution)/shard_map/ppermute | solution.py:23
  60.6 3.8 collective-permute-start.10
  64.4 1.5 collective-permute-start.11
  66.0 2.1 collective-permute-done.10
  68.1 5.4 %collective-permute-done.11 = f32[6,20,2,132]{3,2,1,0:T(2,128)S(1)} collective-permute-done((f32[6,20,2,132]{3,2,1,0:T(2,128)S(1)}, f32[6,20,2,132]{3,2,1,0:T(2,128)S(1)}, u32[]{:S(2)}, u32[]{:S(2)}) %collective-permute-start.11) | collective-permute-done | bytes 126752 | tf_op jit(solution)/shard_map/ppermute | solution.py:23
  78.4 1.5 fusion.117
  80.0 259.2 %all-reduce.3.cloned.1.call-done = f32[256,256]{0,1:T(8,128)} async-done(((f32[256,256]{0,1:T(8,128)}), f32[256,256]{0,1:T(8,128)}) %all-reduce.3.cloned.1.call-update) | async-done | bytes 262160 | tf_op jit(solution)/shard_map/psum | solution.py:104
  341.3 11.7 %cholesky.50 = f32[128,128]{1,0:T(8,128)S(1)} custom-call(f32[128,128]{1,0:T(8,128)S(1)} %cholesky.118), custom_call_target="Cholesky" | custom-call | tf_op jit(solution)/shard_map/cholesky | solution.py:107
  353.1 9.8 %custom-call.11 = f32[1,128,128]{1,2,0:T(8,128)S(1)} custom-call(f32[1,128,128]{2,1,0:T(8,128)S(1)} %get-tuple-element.79), custom_call_target="InvertDiagBlocksLowerTriangular" | custom-call | tf_op jit(solution)/shard_map/cholesky | solution.py:107
  363.4 11.7 %cholesky.105 = f32[128,128]{1,0:T(8,128)S(1)} custom-call(f32[128,128]{1,0:T(8,128)S(1)} %convolution_subtract_fusion.1), custom_call_target="Cholesky" | custom-call | tf_op jit(solution)/shard_map/cholesky | solution.py:107
  377.9 4.0 while.1
  378.5 1.4 bitcast_dynamic-update-slice_fusion.2
  380.5 1.4 bitcast_dynamic-update-slice_fusion.2
  381.9 19.9 %custom-call.12 = f32[2,128,128]{1,2,0:T(8,128)S(1)} custom-call(f32[2,128,128]{2,1,0:T(8,128)S(1)} %get-tuple-element.10), custom_call_target="InvertDiagBlocksLowerTriangular" | custom-call | tf_op jit(solution)/shard_map/triangular_solve | solution.py:108
  (87 shorter events, 34.8 us)
Async XLA Ops:
  7.2 332.0 %all-reduce.3.cloned.1.call-start = ((), (), s32[]{:S(2)}) async-start(), calls=%async_computation | async-start | bytes 524288 | tf_op jit(solution)/shard_map/psum | solution.py:104
  9.3 4.9 %collective-permute-start = (f32[6,16,16,2]{2,1,3,0:T(8,128)S(1)}, f32[6,16,16,2]{2,1,3,0:T(8,128)S(1)}, u32[]{:S(2)}, u32[]{:S(2)}) collective-permute-start(f32[6,16,16,2]{2,1,3,0:T(8,128)S(1)} %copy.55), channel_id=1, source_target_pairs={{0,1},{1,2},{2,3},{3,0},{4,5},{5,6},{6,7},{7,4},{8,9},{9,10},{10,1... | collective-permute-start | bytes 36872 | tf_op jit(solution)/shard_map/ppermute | solution.py:20
  11.5 4.7 %collective-permute-start.1 = (f32[6,16,16,2]{2,1,3,0:T(8,128)S(1)}, f32[6,16,16,2]{2,1,3,0:T(8,128)S(1)}, u32[]{:S(2)}, u32[]{:S(2)}) collective-permute-start(f32[6,16,16,2]{2,1,3,0:T(8,128)S(1)} %copy.56), channel_id=1, source_target_pairs={{1,0},{2,1},{3,2},{0,3},{5,4},{6,5},{7,6},{4,7},{9,8},{10,9},{11,1... | collective-permute-start | bytes 36872 | tf_op jit(solution)/shard_map/ppermute | solution.py:23
  16.8 12.5 %copy-start.4 = (s32[16,16,128]{2,1,0:T(8,128)S(1)}, s32[16,16,128]{2,1,0:T(8,128)}, u32[]{:S(2)}) copy-start(s32[16,16,128]{2,1,0:T(8,128)} %param.7) | copy-start | bytes 393220
  17.0 2.6 collective-permute-start.2
  18.4 5.1 %collective-permute-start.3 = (f32[6,2,16,132]{3,2,1,0:T(8,128)S(1)}, f32[6,2,16,132]{3,2,1,0:T(8,128)S(1)}, u32[]{:S(2)}, u32[]{:S(2)}) collective-permute-start(f32[6,2,16,132]{3,2,1,0:T(8,128)S(1)} %get-tuple-element.57), channel_id=1, source_target_pairs={{32,0},{64,32},{96,64},{128,96},{160,128},{192,160},{224,192},{33,... | collective-permute-start | bytes 304136 | tf_op jit(solution)/shard_map/ppermute | solution.py:23
  24.2 7.5 %collective-permute-start.4 = (f32[6,20,2,132]{3,2,1,0:T(2,128)S(1)}, f32[6,20,2,132]{3,2,1,0:T(2,128)S(1)}, u32[]{:S(2)}, u32[]{:S(2)}) collective-permute-start(f32[6,20,2,132]{3,2,1,0:T(2,128)S(1)} %get-tuple-element.51), channel_id=1, source_target_pairs={{0,4},{4,8},{8,12},{12,16},{16,20},{20,24},{24,28},{1,5},{5,9},{9,... | collective-permute-start | bytes 380168 | tf_op jit(solution)/shard_map/ppermute | solution.py:20
  28.0 8.1 %collective-permute-start.5 = (f32[6,20,2,132]{3,2,1,0:T(2,128)S(1)}, f32[6,20,2,132]{3,2,1,0:T(2,128)S(1)}, u32[]{:S(2)}, u32[]{:S(2)}) collective-permute-start(f32[6,20,2,132]{3,2,1,0:T(2,128)S(1)} %get-tuple-element.52), channel_id=1, source_target_pairs={{4,0},{8,4},{12,8},{16,12},{20,16},{24,20},{28,24},{5,1},{9,5},{13... | collective-permute-start | bytes 380168 | tf_op jit(solution)/shard_map/ppermute | solution.py:23
  37.9 1.2 copy-start
  38.6 1.0 copy-start.3
  41.5 4.7 %collective-permute-start.6 = (f32[6,16,16,2]{2,1,3,0:T(8,128)S(1)}, f32[6,16,16,2]{2,1,3,0:T(8,128)S(1)}, u32[]{:S(2)}, u32[]{:S(2)}) collective-permute-start(f32[6,16,16,2]{2,1,3,0:T(8,128)S(1)} %copy.59), channel_id=1, source_target_pairs={{0,1},{1,2},{2,3},{3,0},{4,5},{5,6},{6,7},{7,4},{8,9},{9,10},{10,1... | collective-permute-start | bytes 36872 | tf_op jit(solution)/shard_map/ppermute | solution.py:20
  43.3 4.7 %collective-permute-start.7 = (f32[6,16,16,2]{2,1,3,0:T(8,128)S(1)}, f32[6,16,16,2]{2,1,3,0:T(8,128)S(1)}, u32[]{:S(2)}, u32[]{:S(2)}) collective-permute-start(f32[6,16,16,2]{2,1,3,0:T(8,128)S(1)} %copy.60), channel_id=1, source_target_pairs={{1,0},{2,1},{3,2},{0,3},{5,4},{6,5},{7,6},{4,7},{9,8},{10,9},{11,1... | collective-permute-start | bytes 36872 | tf_op jit(solution)/shard_map/ppermute | solution.py:23
  48.7 17.2 %copy-start.5 = (s32[16,16,1]{1,2,0:T(1,128)S(1)}, s32[16,16,1]{1,2,0:T(1,128)}, u32[]{:S(2)}) copy-start(s32[16,16,1]{1,2,0:T(1,128)} %param.8) | copy-start | bytes 3076
  48.9 4.8 %collective-permute-start.8 = (f32[6,2,16,132]{3,2,1,0:T(8,128)S(1)}, f32[6,2,16,132]{3,2,1,0:T(8,128)S(1)}, u32[]{:S(2)}, u32[]{:S(2)}) collective-permute-start(f32[6,2,16,132]{3,2,1,0:T(8,128)S(1)} %get-tuple-element.54), channel_id=1, source_target_pairs={{0,32},{32,64},{64,96},{96,128},{128,160},{160,192},{192,224},{1,3... | collective-permute-start | bytes 304136 | tf_op jit(solution)/shard_map/ppermute | solution.py:20
  52.3 7.6 %collective-permute-start.9 = (f32[6,2,16,132]{3,2,1,0:T(8,128)S(1)}, f32[6,2,16,132]{3,2,1,0:T(8,128)S(1)}, u32[]{:S(2)}, u32[]{:S(2)}) collective-permute-start(f32[6,2,16,132]{3,2,1,0:T(8,128)S(1)} %get-tuple-element.55), channel_id=1, source_target_pairs={{32,0},{64,32},{96,64},{128,96},{160,128},{192,160},{224,192},{33,... | collective-permute-start | bytes 304136 | tf_op jit(solution)/shard_map/ppermute | solution.py:23
  60.6 7.5 %collective-permute-start.10 = (f32[6,20,2,132]{3,2,1,0:T(2,128)S(1)}, f32[6,20,2,132]{3,2,1,0:T(2,128)S(1)}, u32[]{:S(2)}, u32[]{:S(2)}) collective-permute-start(f32[6,20,2,132]{3,2,1,0:T(2,128)S(1)} %get-tuple-element.49), channel_id=1, source_target_pairs={{0,4},{4,8},{8,12},{12,16},{16,20},{20,24},{24,28},{1,5},{5,9},{9,... | collective-permute-start | bytes 380168 | tf_op jit(solution)/shard_map/ppermute | solution.py:20
  64.4 9.1 %collective-permute-start.11 = (f32[6,20,2,132]{3,2,1,0:T(2,128)S(1)}, f32[6,20,2,132]{3,2,1,0:T(2,128)S(1)}, u32[]{:S(2)}, u32[]{:S(2)}) collective-permute-start(f32[6,20,2,132]{3,2,1,0:T(2,128)S(1)} %get-tuple-element.50), channel_id=1, source_target_pairs={{4,0},{8,4},{12,8},{16,12},{20,16},{24,20},{28,24},{5,1},{9,5},{13... | collective-permute-start | bytes 380168 | tf_op jit(solution)/shard_map/ppermute | solution.py:23
  75.1 1.5 copy-start.1
  76.6 1.6 copy-start.2
Sparse Core Ops, SparseCore 0:
  80.1 259.0 all-reduce.2
where the time goes:
time: 413 us; the launch traced here: 412 us
  waiting for transfers between devices  290 us (70%)
  other arithmetic  67.8 us (16%)
  starting transfers between devices  22.3 us (5%)
  between operations  15.7 us (4%)
  local copies, waits for them, and re-layouts  12.8 us (3%)
    psum x1, waiting for transfers between devices, on_device(): lax.psum(jnp.dot(matrix, matrix.T, precision=lax.Precision.HIGHEST), ('ro...  259 us
    another operation x7, other arithmetic, on_device(): factor_low = lax.linalg.cholesky(gram_sum)  34.6 us
    ppermute x6, waiting for transfers between devices, with_halo(): lax.ppermute(lax.slice_in_dim(block, 0, width, axis=dim), axis, backward)  22.4 us
    another operation x2, other arithmetic, on_device(): lax.linalg.triangular_solve(factor_low, matrix, left_side=True, lower=True)  19.9 us
    ppermute x6, starting transfers between devices, with_halo(): lax.ppermute(lax.slice_in_dim(block, block.shape[dim] - width, None, axis...  15.2 us
  transfers between devices with their start and end apart: 13, of which 11 were waited for; matrix products, arithmetic and copies ran while one was open for 1% of the time, Pallas kernels for 0%

commit v1 on v0

--- a/solution.py
+++ b/solution.py
@@ -1,13 +1,24 @@
+import functools
 import math
 import jax
 import jax.numpy as jnp
 from jax import lax
 from jax.sharding import PartitionSpec as P
+from jax.lax import psum
 
 SPACING = 128
 damping_rate = 3.0
 time_step = 0.3
 azimuth_gain = 5.0
+
+
+def zones_cut(load, device_axis, shard_axis):
+    for to_i in (device_axis, shard_axis):
+        load = psum(load, axis_name=to_i)
+    return load
+
+
+kinds_take = functools.partial(zones_cut, device_axis=("th", "ph"), shard_axis="row")
 
 
 def with_halo(block, sides, width, periodic):
@@ -101,9 +112,7 @@
         ]
     )
     matrix = jnp.concatenate([old_basis, snapshot], axis=0)
-    gram_sum = lax.psum(
-        jnp.dot(matrix, matrix.T, precision=lax.Precision.HIGHEST), ("row", "th", "ph")
-    )
+    gram_sum = kinds_take(jnp.dot(matrix, matrix.T, precision=lax.Precision.HIGHEST))
     factor_low = lax.linalg.cholesky(gram_sum)
     solved = lax.linalg.triangular_solve(factor_low, matrix, left_side=True, lower=True)
     row_scale = math.sqrt(

time: 413 us -> 368 us (0.89)
  waiting for transfers between devices: 290 us -> 246 us
    psum x1 -> x2, waiting for transfers between devices: 259 us -> 215 us  [zones_cut(): load = psum(load, axis_name=to_i)]
  transfers between devices with their start and end apart: 13 -> 14, of which waited for: 11 -> 12; matrix products, arithmetic and copies ran while one was open for 1% -> 1% of each run, Pallas kernels for 0% -> 0%
where the time goes in v1:
time: 368 us
  waiting for transfers between devices  246 us (67%)
  other arithmetic  67.6 us (18%)
  starting transfers between devices  22.3 us (6%)
  between operations  15.7 us (4%)
  local copies, waits for them, and re-layouts  12.8 us (3%)
    psum x2, waiting for transfers between devices, zones_cut(): load = psum(load, axis_name=to_i)  215 us
    another operation x7, other arithmetic, on_device(): factor_low = lax.linalg.cholesky(gram_sum)  34.6 us
    ppermute x6, waiting for transfers between devices, with_halo(): lax.ppermute(lax.slice_in_dim(block, 0, width, axis=dim), axis, backward)  22.4 us
    another operation x2, other arithmetic, on_device(): lax.linalg.triangular_solve(factor_low, matrix, left_side=True, lower=True)  19.7 us
    ppermute x6, starting transfers between devices, with_halo(): lax.ppermute(lax.slice_in_dim(block, block.shape[dim] - width, None, axis...  15.2 us
    ppermute x6, waiting for transfers between devices, with_halo(): lax.ppermute(lax.slice_in_dim(block, block.shape[dim] - width, None, axis...  8.16 us
  transfers between devices with their start and end apart: 14, of which 12 were waited for; matrix products, arithmetic and copies ran while one was open for 1% of the time, Pallas kernels for 0%

profile of v1, /device:TPU:2, one launch (start us, length us, event | category | flops | bytes accessed | tf_op | source)
XLA Modules:
  0.0 367.8 jit_solution(4200919090052524463)
XLA Ops:
  9.3 1.6 collective-permute-start
  12.3 1.9 collective-permute-done
  14.9 1.3 collective-permute-done.1
  19.7 3.8 %collective-permute-done.3 = f32[6,2,16,132]{3,2,1,0:T(8,128)S(1)} collective-permute-done((f32[6,2,16,132]{3,2,1,0:T(8,128)S(1)}, f32[6,2,16,132]{3,2,1,0:T(8,128)S(1)}, u32[]{:S(2)}, u32[]{:S(2)}) %collective-permute-start.3) | collective-permute-done | bytes 101408 | tf_op jit(solution)/shard_map/ppermute | solution.py:34
  24.2 3.8 %collective-permute-start.4 = (f32[6,20,2,132]{3,2,1,0:T(2,128)S(1)}, f32[6,20,2,132]{3,2,1,0:T(2,128)S(1)}, u32[]{:S(2)}, u32[]{:S(2)}) collective-permute-start(f32[6,20,2,132]{3,2,1,0:T(2,128)S(1)} %get-tuple-element.51), channel_id=1, source_target_pairs={{0,4},{4,8},{8,12},{12,16},{16,20},{20,24},{24,28},{1,5},{5,9},{9,... | collective-permute-start | bytes 380168 | tf_op jit(solution)/shard_map/ppermute | solution.py:31
  29.3 2.4 collective-permute-done.4
  31.7 4.4 %collective-permute-done.5 = f32[6,20,2,132]{3,2,1,0:T(2,128)S(1)} collective-permute-done((f32[6,20,2,132]{3,2,1,0:T(2,128)S(1)}, f32[6,20,2,132]{3,2,1,0:T(2,128)S(1)}, u32[]{:S(2)}, u32[]{:S(2)}) %collective-permute-start.5) | collective-permute-done | bytes 126752 | tf_op jit(solution)/shard_map/ppermute | solution.py:34
  44.3 1.9 collective-permute-done.6
  48.9 3.4 collective-permute-start.8
  53.6 6.2 %collective-permute-done.9 = f32[6,2,16,132]{3,2,1,0:T(8,128)S(1)} collective-permute-done((f32[6,2,16,132]{3,2,1,0:T(8,128)S(1)}, f32[6,2,16,132]{3,2,1,0:T(8,128)S(1)}, u32[]{:S(2)}, u32[]{:S(2)}) %collective-permute-start.9) | collective-permute-done | bytes 101408 | tf_op jit(solution)/shard_map/ppermute | solution.py:34
  60.6 3.8 %collective-permute-start.10 = (f32[6,20,2,132]{3,2,1,0:T(2,128)S(1)}, f32[6,20,2,132]{3,2,1,0:T(2,128)S(1)}, u32[]{:S(2)}, u32[]{:S(2)}) collective-permute-start(f32[6,20,2,132]{3,2,1,0:T(2,128)S(1)} %get-tuple-element.49), channel_id=1, source_target_pairs={{0,4},{4,8},{8,12},{12,16},{16,20},{20,24},{24,28},{1,5},{5,9},{9,... | collective-permute-start | bytes 380168 | tf_op jit(solution)/shard_map/ppermute | solution.py:31
  64.4 1.5 collective-permute-start.11
  66.0 2.1 collective-permute-done.10
  68.1 5.4 %collective-permute-done.11 = f32[6,20,2,132]{3,2,1,0:T(2,128)S(1)} collective-permute-done((f32[6,20,2,132]{3,2,1,0:T(2,128)S(1)}, f32[6,20,2,132]{3,2,1,0:T(2,128)S(1)}, u32[]{:S(2)}, u32[]{:S(2)}) %collective-permute-start.11) | collective-permute-done | bytes 126752 | tf_op jit(solution)/shard_map/ppermute | solution.py:34
  78.4 1.5 fusion.117
  80.0 149.0 %all-reduce.4.cloned.1.call-done = f32[256,256]{0,1:T(8,128)} async-done(((f32[256,256]{0,1:T(8,128)}), f32[256,256]{0,1:T(8,128)}) %all-reduce.4.cloned.1.call-update) | async-done | bytes 262160 | tf_op jit(solution)/shard_map/psum | solution.py:17
  229.1 66.0 %all-reduce.6.cloned.1.call-done = f32[256,256]{0,1:T(8,128)} async-done(((f32[256,256]{0,1:T(8,128)}), f32[256,256]{0,1:T(8,128)}) %all-reduce.6.cloned.1.call-update) | async-done | bytes 262160 | tf_op jit(solution)/shard_map/psum | solution.py:17
  297.2 11.7 %cholesky.50 = f32[128,128]{1,0:T(8,128)S(1)} custom-call(f32[128,128]{1,0:T(8,128)S(1)} %cholesky.118), custom_call_target="Cholesky" | custom-call | tf_op jit(solution)/shard_map/cholesky | solution.py:116
  308.9 9.8 %custom-call.11 = f32[1,128,128]{1,2,0:T(8,128)S(1)} custom-call(f32[1,128,128]{2,1,0:T(8,128)S(1)} %get-tuple-element.79), custom_call_target="InvertDiagBlocksLowerTriangular" | custom-call | tf_op jit(solution)/shard_map/cholesky | solution.py:116
  319.2 11.7 %cholesky.105 = f32[128,128]{1,0:T(8,128)S(1)} custom-call(f32[128,128]{1,0:T(8,128)S(1)} %convolution_subtract_fusion.1), custom_call_target="Cholesky" | custom-call | tf_op jit(solution)/shard_map/cholesky | solution.py:116
  333.8 4.2 %while.1 = (s32[]{:T(128)}, f32[256,256]{1,0:T(8,128)S(1)}, s32[2,2]{1,0:T(2,128)S(1)}, f32[2,128,128]{2,1,0:T(8,128)S(1)}, s32[]{:T(128)}) while((s32[]{:T(128)}, f32[256,256]{1,0:T(8,128)S(1)}, s32[2,2]{1,0:T(2,128)S(1)}, f32[2,128,128]{2,1,0:T(8,128)S(1)}, s32[]{:T(128)}) %tuple.61), condition=%wide.while_cond, body=%wide.while_body.sunk | while | flops 2 | bytes 131181 | solution.py:117
  334.5 1.4 bitcast_dynamic-update-slice_fusion.2
  336.6 1.4 bitcast_dynamic-update-slice_fusion.2
  338.0 19.7 %custom-call.12 = f32[2,128,128]{1,2,0:T(8,128)S(1)} custom-call(f32[2,128,128]{2,1,0:T(8,128)S(1)} %get-tuple-element.10), custom_call_target="InvertDiagBlocksLowerTriangular" | custom-call | tf_op jit(solution)/shard_map/triangular_solve | solution.py:117
  (90 shorter events, 36.2 us)
Async XLA Ops:
  7.2 221.9 %all-reduce.4.cloned.1.call-start = ((), (), s32[]{:S(2)}) async-start(), calls=%async_computation | async-start | bytes 524288 | tf_op jit(solution)/shard_map/psum | solution.py:17
  9.3 4.9 %collective-permute-start = (f32[6,16,16,2]{2,1,3,0:T(8,128)S(1)}, f32[6,16,16,2]{2,1,3,0:T(8,128)S(1)}, u32[]{:S(2)}, u32[]{:S(2)}) collective-permute-start(f32[6,16,16,2]{2,1,3,0:T(8,128)S(1)} %copy.55), channel_id=1, source_target_pairs={{0,1},{1,2},{2,3},{3,0},{4,5},{5,6},{6,7},{7,4},{8,9},{9,10},{10,1... | collective-permute-start | bytes 36872 | tf_op jit(solution)/shard_map/ppermute | solution.py:31
  11.5 4.7 %collective-permute-start.1 = (f32[6,16,16,2]{2,1,3,0:T(8,128)S(1)}, f32[6,16,16,2]{2,1,3,0:T(8,128)S(1)}, u32[]{:S(2)}, u32[]{:S(2)}) collective-permute-start(f32[6,16,16,2]{2,1,3,0:T(8,128)S(1)} %copy.56), channel_id=1, source_target_pairs={{1,0},{2,1},{3,2},{0,3},{5,4},{6,5},{7,6},{4,7},{9,8},{10,9},{11,1... | collective-permute-start | bytes 36872 | tf_op jit(solution)/shard_map/ppermute | solution.py:34
  16.8 12.5 %copy-start.4 = (s32[16,16,128]{2,1,0:T(8,128)S(1)}, s32[16,16,128]{2,1,0:T(8,128)}, u32[]{:S(2)}) copy-start(s32[16,16,128]{2,1,0:T(8,128)} %param.7) | copy-start | bytes 393220
  17.0 2.6 collective-permute-start.2
  18.4 5.1 %collective-permute-start.3 = (f32[6,2,16,132]{3,2,1,0:T(8,128)S(1)}, f32[6,2,16,132]{3,2,1,0:T(8,128)S(1)}, u32[]{:S(2)}, u32[]{:S(2)}) collective-permute-start(f32[6,2,16,132]{3,2,1,0:T(8,128)S(1)} %get-tuple-element.57), channel_id=1, source_target_pairs={{32,0},{64,32},{96,64},{128,96},{160,128},{192,160},{224,192},{33,... | collective-permute-start | bytes 304136 | tf_op jit(solution)/shard_map/ppermute | solution.py:34
  24.2 7.5 %collective-permute-start.4 = (f32[6,20,2,132]{3,2,1,0:T(2,128)S(1)}, f32[6,20,2,132]{3,2,1,0:T(2,128)S(1)}, u32[]{:S(2)}, u32[]{:S(2)}) collective-permute-start(f32[6,20,2,132]{3,2,1,0:T(2,128)S(1)} %get-tuple-element.51), channel_id=1, source_target_pairs={{0,4},{4,8},{8,12},{12,16},{16,20},{20,24},{24,28},{1,5},{5,9},{9,... | collective-permute-start | bytes 380168 | tf_op jit(solution)/shard_map/ppermute | solution.py:31
  28.0 8.1 %collective-permute-start.5 = (f32[6,20,2,132]{3,2,1,0:T(2,128)S(1)}, f32[6,20,2,132]{3,2,1,0:T(2,128)S(1)}, u32[]{:S(2)}, u32[]{:S(2)}) collective-permute-start(f32[6,20,2,132]{3,2,1,0:T(2,128)S(1)} %get-tuple-element.52), channel_id=1, source_target_pairs={{4,0},{8,4},{12,8},{16,12},{20,16},{24,20},{28,24},{5,1},{9,5},{13... | collective-permute-start | bytes 380168 | tf_op jit(solution)/shard_map/ppermute | solution.py:34
  37.9 1.2 copy-start
  38.6 1.0 copy-start.3
  41.5 4.7 %collective-permute-start.6 = (f32[6,16,16,2]{2,1,3,0:T(8,128)S(1)}, f32[6,16,16,2]{2,1,3,0:T(8,128)S(1)}, u32[]{:S(2)}, u32[]{:S(2)}) collective-permute-start(f32[6,16,16,2]{2,1,3,0:T(8,128)S(1)} %copy.59), channel_id=1, source_target_pairs={{0,1},{1,2},{2,3},{3,0},{4,5},{5,6},{6,7},{7,4},{8,9},{9,10},{10,1... | collective-permute-start | bytes 36872 | tf_op jit(solution)/shard_map/ppermute | solution.py:31
  43.3 4.7 %collective-permute-start.7 = (f32[6,16,16,2]{2,1,3,0:T(8,128)S(1)}, f32[6,16,16,2]{2,1,3,0:T(8,128)S(1)}, u32[]{:S(2)}, u32[]{:S(2)}) collective-permute-start(f32[6,16,16,2]{2,1,3,0:T(8,128)S(1)} %copy.60), channel_id=1, source_target_pairs={{1,0},{2,1},{3,2},{0,3},{5,4},{6,5},{7,6},{4,7},{9,8},{10,9},{11,1... | collective-permute-start | bytes 36872 | tf_op jit(solution)/shard_map/ppermute | solution.py:34
  48.7 17.2 %copy-start.5 = (s32[16,16,1]{1,2,0:T(1,128)S(1)}, s32[16,16,1]{1,2,0:T(1,128)}, u32[]{:S(2)}) copy-start(s32[16,16,1]{1,2,0:T(1,128)} %param.8) | copy-start | bytes 3076
  48.9 4.8 %collective-permute-start.8 = (f32[6,2,16,132]{3,2,1,0:T(8,128)S(1)}, f32[6,2,16,132]{3,2,1,0:T(8,128)S(1)}, u32[]{:S(2)}, u32[]{:S(2)}) collective-permute-start(f32[6,2,16,132]{3,2,1,0:T(8,128)S(1)} %get-tuple-element.54), channel_id=1, source_target_pairs={{0,32},{32,64},{64,96},{96,128},{128,160},{160,192},{192,224},{1,3... | collective-permute-start | bytes 304136 | tf_op jit(solution)/shard_map/ppermute | solution.py:31
  52.3 7.6 %collective-permute-start.9 = (f32[6,2,16,132]{3,2,1,0:T(8,128)S(1)}, f32[6,2,16,132]{3,2,1,0:T(8,128)S(1)}, u32[]{:S(2)}, u32[]{:S(2)}) collective-permute-start(f32[6,2,16,132]{3,2,1,0:T(8,128)S(1)} %get-tuple-element.55), channel_id=1, source_target_pairs={{32,0},{64,32},{96,64},{128,96},{160,128},{192,160},{224,192},{33,... | collective-permute-start | bytes 304136 | tf_op jit(solution)/shard_map/ppermute | solution.py:34
  60.6 7.5 %collective-permute-start.10 = (f32[6,20,2,132]{3,2,1,0:T(2,128)S(1)}, f32[6,20,2,132]{3,2,1,0:T(2,128)S(1)}, u32[]{:S(2)}, u32[]{:S(2)}) collective-permute-start(f32[6,20,2,132]{3,2,1,0:T(2,128)S(1)} %get-tuple-element.49), channel_id=1, source_target_pairs={{0,4},{4,8},{8,12},{12,16},{16,20},{20,24},{24,28},{1,5},{5,9},{9,... | collective-permute-start | bytes 380168 | tf_op jit(solution)/shard_map/ppermute | solution.py:31
  64.4 9.1 %collective-permute-start.11 = (f32[6,20,2,132]{3,2,1,0:T(2,128)S(1)}, f32[6,20,2,132]{3,2,1,0:T(2,128)S(1)}, u32[]{:S(2)}, u32[]{:S(2)}) collective-permute-start(f32[6,20,2,132]{3,2,1,0:T(2,128)S(1)} %get-tuple-element.50), channel_id=1, source_target_pairs={{4,0},{8,4},{12,8},{16,12},{20,16},{24,20},{28,24},{5,1},{9,5},{13... | collective-permute-start | bytes 380168 | tf_op jit(solution)/shard_map/ppermute | solution.py:34
  75.1 1.5 copy-start.1
  76.6 1.6 copy-start.2
  79.9 215.1 %all-reduce.6.cloned.1.call-start = ((), (), s32[]{:S(2)}) async-start(), calls=%async_computation.1 | async-start | bytes 524288 | tf_op jit(solution)/shard_map/psum | solution.py:17
Sparse Core Ops, SparseCore 0:
  80.1 148.9 all-reduce.3
  231.3 63.6 all-reduce.5
